TPU v7x, 32 devices: a whole 2x2x4 slice. The times are simulated.
32 devices in a mesh: row: 8 (over z, y), col: 4 (over x, core).
Axes of the slice: x: 2, y: 2, z: 4, core: 2. Of those that a mesh axis runs over, the one named last changes fastest.
Arguments:
- field: float32 [512, 64, 8, 512], P('row', 'col'), may hold values from -6 to 6
- modes: int32 [3, 256], replicated, may hold values from 0 to 511, as said below
Outputs:
- spectrum: float32 [64, 512, 8, 512], P(None, 'col', None, 'row')
- localized: float32 [512, 512], replicated
Inputs may be any that keep to these rules, and one draw needn't show every extreme that they name: `modes`: row 0 holds kx in 0 to 255, row 1 ky in 0 to 511, row 2 kz in 0 to 63; triples may repeat.
All inputs are finite; a program needn't handle non-finite values.
Results may differ from a plain program's by a relative error of at most 0.00013.
Values sent between devices are 32-bit elements; how exact they have to be, the bound alone decides.
A program may use at most 192 MiB of HBM per device.

v0:
```python
import math

import jax
import jax.numpy as jnp
from jax import lax
from jax.experimental.layout import Layout, with_layout_constraint
from jax.sharding import PartitionSpec as P

NX = 512
NY = 512
NZ = 64
REACH = 64


highest = lax.Precision.HIGHEST
high = lax.Precision.HIGH
PIECES = 2


def tables(length, count):
    points = lax.iota(jnp.int32, length)
    waves = lax.iota(jnp.int32, count)
    phase = points[:, None] * waves[None, :] % length
    angle = phase.astype(jnp.float32) * (2.0 * math.pi / length)
    return (jnp.cos(angle), jnp.sin(angle))


def taper_of(modes, size_y, size_z, reach):
    first = modes[0].astype(jnp.float32)
    second = jnp.where(modes[1] < size_y // 2, modes[1], modes[1] - size_y).astype(jnp.float32)
    third = jnp.where(modes[2] < size_z // 2, modes[2], modes[2] - size_z).astype(jnp.float32)
    first = jnp.concatenate([first, first])
    second = jnp.concatenate([second, second])
    third = jnp.concatenate([third, third])
    dist = (first[:, None] - first[None, :]) ** 2 + (second[:, None] - second[None, :]) ** 2
    dist = dist + (third[:, None] - third[None, :]) ** 2
    return jnp.exp(-dist / (2.0 * reach * reach))


def twiddle(length, count, scale):
    cos, sin = tables(length, count)
    cos, sin = cos * scale, sin * scale
    return jnp.stack([jnp.stack([cos, sin]), jnp.stack([-sin, cos])])


def per_device(field, modes):
    members = field.shape[2]
    width = field.shape[3]
    rows, cols = lax.axis_size("row"), lax.axis_size("col")
    near, thick = field.shape[0], field.shape[1]
    length, depth = near * rows, thick * cols
    waves = width // 2 // rows
    pieces = PIECES if waves % PIECES == 0 else 1
    part = waves // pieces
    local_y = length // cols
    factor = 1.0 / math.sqrt(NX * NY * NZ)
    cos_x, sin_x = tables(width, width // 2)
    x_table = jnp.stack([cos_x, -sin_x]).reshape(2, width, rows, pieces, part)
    y_table = twiddle(length, length, 1.0).reshape(2, 2, rows, near, length)
    z_table = twiddle(depth, depth, factor).reshape(2, 2, cols, thick, depth)
    flat = field.reshape(near, thick * members, width)
    outs = []
    for piece in range(pieces):
        lines = jnp.einsum("cxrk,ylx->rckyl", x_table[:, :, :, piece], flat, precision=high)
        lines = with_layout_constraint(lines, Layout((0, 1, 2, 3, 4)))
        gathered = lax.all_to_all(lines, "row", split_axis=0, concat_axis=0, tiled=True)
        gathered = with_layout_constraint(gathered, Layout((0, 1, 2, 3, 4)))
        gathered = gathered.reshape(rows, 2, part, near, thick, members)
        ytrans = jnp.einsum("dcsyf,sckyzm->dkmzf", y_table, gathered, precision=high)
        ytrans = ytrans.reshape(2, part, members, thick, cols, local_y)
        ytrans = jnp.transpose(ytrans, (4, 0, 1, 2, 3, 5))
        levels = lax.all_to_all(ytrans, "col", split_axis=0, concat_axis=0, tiled=True)
        outs.append(jnp.einsum("edszg,sdkmzf->gmkef", z_table, levels, precision=high))
    whole = jnp.concatenate(outs, axis=2) if pieces > 1 else outs[0]
    local_q = 2 * waves
    whole = whole.reshape(depth, members, local_q, local_y)
    spectrum = jnp.transpose(whole, (0, 3, 1, 2))
    row_start = lax.axis_index("row") * waves
    col_start = lax.axis_index("col") * local_y
    wave = modes[0] - row_start
    line = modes[1] - col_start
    inside = (wave >= 0) & (wave < waves) & (line >= 0) & (line < local_y)
    wave = jnp.clip(wave, 0, waves - 1)
    line = jnp.clip(line, 0, local_y - 1)
    columns = lax.iota(jnp.int32, local_y)
    tall = whole.reshape(depth, members, waves, 2, local_y)
    picked = tall[modes[2], :, wave]
    hit = (columns[None, :] == line[:, None]) & inside[:, None]
    value = jnp.sum(jnp.where(hit[:, None, None, :], picked, 0.0), axis=-1)
    partial_value = jnp.transpose(value, (1, 2, 0)).reshape(members, -1)
    coef = lax.psum(partial_value, ("row", "col"))
    anomaly = coef - jnp.mean(coef, axis=0, keepdims=True)
    cov = jnp.dot(anomaly.T, anomaly, precision=highest) / (members - 1)
    localized = cov * taper_of(modes, NY, NZ, REACH)
    return (spectrum, localized)


def solution(mesh):
    placed = (P("row", "col", None, None), P())
    return jax.shard_map(
        per_device,
        mesh=mesh,
        in_specs=placed,
        out_specs=(P(None, "col", None, "row"), P()),
        check_vma=False,
    )
```

profile of v0, /device:TPU:0, one launch (start us, length us, event | category | flops | bytes accessed | tf_op | source)
XLA Modules:
  0.0 698.6 jit_solution(1257400286542088055)
XLA Ops:
  0.6 2.1 fusion.34
  2.8 10.2 %fusion.4 = f32[2,8,16,64,128]{4,2,3,1,0:T(8,128)S(1)} fusion(f32[64,16,8,512]{3,2,1,0:T(8,128)} %param.2, f32[1,512,8,2,16]{1,4,2,0,3:T(8,128)S(1)} %get-tuple-element.6, f32[1,512,8,2,16]{1,4,2,0,3:T(8,128)S(1)} %get-tuple-element.7), kind=kOutput, calls=%fused_computation.6 | convolution fusion | flops 6442582016 | bytes 26214400 | tf_op jit(solution)/shard_map/cxrk,ylx->rckyl/dot_general | solution.py:64
  13.0 6.0 copy.83
  19.0 7.6 %all-to-all-start = ((f32[8,2,16,64,128]{4,3,2,1,0:T(8,128)}), f32[8,2,16,64,128]{4,3,2,1,0:T(8,128)}, u32[]{:S(2)}, u32[]{:S(2)}) async-start(f32[8,2,16,64,128]{4,3,2,1,0:T(8,128)} %bitcast.107), calls=%async_computation | async-start | bytes 16777216 | tf_op jit(solution)/shard_map/all_to_all | solution.py:66
  26.6 10.2 %fusion.2 = f32[2,8,16,64,128]{4,2,3,1,0:T(8,128)S(1)} fusion(f32[64,16,8,512]{3,2,1,0:T(8,128)} %param.2, f32[1,512,8,2,16]{1,4,2,0,3:T(8,128)S(1)} %get-tuple-element.7, f32[1,512,8,2,16]{1,4,2,0,3:T(8,128)S(1)} %get-tuple-element.6), kind=kOutput, calls=%fused_computation.4 | convolution fusion | flops 6442582016 | bytes 26214400 | tf_op jit(solution)/shard_map/cxrk,ylx->rckyl/dot_general | solution.py:64
  36.9 5.8 copy.81
  42.7 167.0 %all-to-all-done = f32[8,2,16,64,128]{4,3,2,1,0:T(8,128)} async-done(((f32[8,2,16,64,128]{4,3,2,1,0:T(8,128)}), f32[8,2,16,64,128]{4,3,2,1,0:T(8,128)}, u32[]{:S(2)}, u32[]{:S(2)}) %all-to-all-start) | async-done | bytes 8388640 | tf_op jit(solution)/shard_map/all_to_all | solution.py:66
  209.7 5.3 all-to-all-start.2
  215.0 4.2 fusion.28
  219.2 12.2 %copy.22 = f32[8,2,16,64,128]{3,4,2,1,0:T(8,128)} copy(f32[8,2,16,64,128]{4,3,2,1,0:T(8,128)} %all-to-all-done) | data formatting | bytes 16777216 | tf_op jit(solution)/shard_map/layout_constraint | solution.py:67
  231.5 27.8 %fusion.6 = f32[16,16,8,2,512,1,1]{4,2,5,1,0,3,6:T(8,128)S(1)} fusion(f32[1,1,8,64,512]{4,3,1,0,2:T(8,128)S(1)} %get-tuple-element.13, f32[1,1,8,64,512]{4,3,1,0,2:T(8,128)S(1)} %get-tuple-element.12, f32[1,1,8,64,512]{4,3,1,0,2:T(8,128)S(1)} %get-tuple-element.11, f32[8,2,16,64,128]{3,4,2,1,0:T(8,128)} %copy.22), kind=kOutput, calls=%fused_computation.8 | convolution fusion | flops 12888047616 | bytes 19922944 | tf_op jit(solution)/shard_map/dcsyf,sckyzm->dkmzf/dot_general | solution.py:69
  259.2 1.4 copy.79
  260.7 8.1 %copy.82 = f32[2,16,8,16,4,128]{5,3,0,2,1,4:T(8,128)} copy(f32[2,16,8,16,4,128]{5,2,4,1,0,3:T(8,128)S(1)} %bitcast.108) | data formatting | bytes 16777216 | tf_op jit(solution)/shard_map/reshape | solution.py:70
  268.7 128.5 %all-to-all-done.2 = f32[8,2,16,64,128]{4,3,2,1,0:T(8,128)} async-done(((f32[8,2,16,64,128]{4,3,2,1,0:T(8,128)}), f32[8,2,16,64,128]{4,3,2,1,0:T(8,128)}, u32[]{:S(2)}, u32[]{:S(2)}) %all-to-all-start.2) | async-done | bytes 8388640 | tf_op jit(solution)/shard_map/all_to_all | solution.py:66
  397.2 5.8 all-to-all-start.1
  403.1 12.2 %copy.27 = f32[8,2,16,64,128]{3,4,2,1,0:T(8,128)} copy(f32[8,2,16,64,128]{4,3,2,1,0:T(8,128)} %all-to-all-done.2) | data formatting | bytes 16777216 | tf_op jit(solution)/shard_map/layout_constraint | solution.py:67
  415.3 27.3 %fusion = f32[16,16,8,2,512,1,1]{4,2,5,1,0,3,6:T(8,128)S(1)} fusion(f32[1,1,8,64,512]{4,3,1,0,2:T(8,128)S(1)} %get-tuple-element.13, f32[1,1,8,64,512]{4,3,1,0,2:T(8,128)S(1)} %get-tuple-element.12, f32[1,1,8,64,512]{4,3,1,0,2:T(8,128)S(1)} %get-tuple-element.11, f32[8,2,16,64,128]{3,4,2,1,0:T(8,128)} %copy.27), kind=kOutput, calls=%fused_computation.2 | convolution fusion | flops 12888047616 | bytes 19922944 | tf_op jit(solution)/shard_map/dcsyf,sckyzm->dkmzf/dot_general | solution.py:69
  442.6 1.4 copy.78
  444.0 8.3 %copy.80 = f32[2,16,8,16,4,128]{5,3,0,2,1,4:T(8,128)} copy(f32[2,16,8,16,4,128]{5,2,4,1,0,3:T(8,128)S(1)} %bitcast.109) | data formatting | bytes 16777216 | tf_op jit(solution)/shard_map/reshape | solution.py:70
  452.3 43.9 %all-to-all-done.1 = f32[4,2,16,8,16,128]{5,4,1,3,2,0:T(8,128)} async-done(((f32[4,2,16,8,16,128]{5,4,1,3,2,0:T(8,128)}), f32[4,2,16,8,16,128]{5,4,1,3,2,0:T(8,128)}, u32[]{:S(2)}, u32[]{:S(2)}) %all-to-all-start.1) | async-done | bytes 8388640 | tf_op jit(solution)/shard_map/all_to_all | solution.py:72
  496.2 6.0 all-to-all-start.3
  502.7 10.2 %fusion.10 = f32[16,8,128,2,64,1,1]{2,4,5,0,3,1,6:T(8,128)} fusion(f32[4,2,16,8,16,128]{5,4,1,3,2,0:T(8,128)} %all-to-all-done.1, f32[1,1,4,16,64]{4,3,2,1,0:T(8,128)S(1)} %get-tuple-element.16, f32[1,1,4,16,64]{4,3,2,1,0:T(8,128)S(1)} %get-tuple-element.15, f32[1,1,4,16,64]{4,3,2,1,0:T(8,128)S(1)} %get-tuple-element.14), kind=kOutput, calls=%fused_computation.12 | convolution fusion | flops 1610661888 | bytes 16826368 | tf_op jit(solution)/shard_map/edszg,sdkmzf->gmkef/dot_general | solution.py:73
  512.9 82.4 %all-to-all-done.3 = f32[4,2,16,8,16,128]{5,4,1,3,2,0:T(8,128)} async-done(((f32[4,2,16,8,16,128]{5,4,1,3,2,0:T(8,128)}), f32[4,2,16,8,16,128]{5,4,1,3,2,0:T(8,128)}, u32[]{:S(2)}, u32[]{:S(2)}) %all-to-all-start.3) | async-done | bytes 8388640 | tf_op jit(solution)/shard_map/all_to_all | solution.py:72
  595.3 6.3 fusion.8
  601.7 7.9 %copy_bitcast_fusion = (f32[64,8,16,2,128]{4,0,3,1,2:T(8,128)}, f32[64,8,16,2,128]{4,0,3,1,2:T(8,128)}) fusion(f32[16,8,128,2,64,1,1]{2,4,5,0,3,1,6:T(8,128)S(1)} %fusion.8, f32[16,8,128,2,64,1,1]{2,4,5,0,3,1,6:T(8,128)S(1)} %copy-done), kind=kLoop, calls=%fused_computation.14 | loop fusion | bytes 33554432 | tf_op jit(solution)/shard_map/edszg,sdkmzf->gmkef/transpose | solution.py:73
  609.6 7.0 pad_maximum_fusion
  616.5 19.5 %copy.31 = f32[64,8,32,2,128]{4,1,3,2,0:T(8,128)} copy(f32[64,8,32,2,128]{4,0,3,1,2:T(8,128)S(1)} %pad_maximum_fusion) | data formatting | bytes 33554432 | tf_op jit(solution)/shard_map/concatenate | solution.py:74
  636.1 6.9 gather_fusion
  643.0 0.9 select_reduce_fusion
  644.0 37.7 %psum.7 = f32[8,512]{1,0:T(8,128)S(1)} all-reduce(f32[8,512]{1,0:T(8,128)S(1)} %bitcast.112), channel_id=1, replica_groups=mesh['row'=8,'col'=4] {'row','col'}, use_global_device_ids=true, to_apply=%region_1.2 | all-reduce | flops 4096 | bytes 32768 | tf_op jit(solution)/shard_map/psum | solution.py:91
  681.7 14.2 %copy.34 = f32[64,128,8,64]{1,3,2,0:T(8,128)} copy(f32[64,128,8,64]{1,2,3,0:T(8,128)} %bitcast.103) | data formatting | bytes 33554432
  695.9 2.3 fusion.12
  (20 shorter events, 0.6 us)
Async XLA Ops:
  19.0 190.7 %all-to-all-start = ((f32[8,2,16,64,128]{4,3,2,1,0:T(8,128)}), f32[8,2,16,64,128]{4,3,2,1,0:T(8,128)}, u32[]{:S(2)}, u32[]{:S(2)}) async-start(f32[8,2,16,64,128]{4,3,2,1,0:T(8,128)} %bitcast.107), calls=%async_computation | async-start | bytes 16777216 | tf_op jit(solution)/shard_map/all_to_all | solution.py:66
  209.7 187.5 %all-to-all-start.2 = ((f32[8,2,16,64,128]{4,3,2,1,0:T(8,128)}), f32[8,2,16,64,128]{4,3,2,1,0:T(8,128)}, u32[]{:S(2)}, u32[]{:S(2)}) async-start(f32[8,2,16,64,128]{4,3,2,1,0:T(8,128)} %bitcast.105), calls=%async_computation.2 | async-start | bytes 16777216 | tf_op jit(solution)/shard_map/all_to_all | solution.py:66
  397.2 98.9 %all-to-all-start.1 = ((f32[4,2,16,8,16,128]{5,4,1,3,2,0:T(8,128)}), f32[4,2,16,8,16,128]{5,4,1,3,2,0:T(8,128)}, u32[]{:S(2)}, u32[]{:S(2)}) async-start(f32[4,2,16,8,16,128]{5,4,1,3,2,0:T(8,128)} %bitcast.106), calls=%async_computation.1 | async-start | bytes 16777216 | tf_op jit(solution)/shard_map/all_to_all | solution.py:72
  496.2 6.0 copy-start.1
  496.2 99.1 %all-to-all-start.3 = ((f32[4,2,16,8,16,128]{5,4,1,3,2,0:T(8,128)}), f32[4,2,16,8,16,128]{5,4,1,3,2,0:T(8,128)}, u32[]{:S(2)}, u32[]{:S(2)}) async-start(f32[4,2,16,8,16,128]{5,4,1,3,2,0:T(8,128)} %bitcast.104), calls=%async_computation.3 | async-start | bytes 16777216 | tf_op jit(solution)/shard_map/all_to_all | solution.py:72
  595.3 6.3 copy-start
where the time goes:
time: 705 us; the launch traced here: 699 us
  waiting for transfers between devices  422 us (60%)
  local copies, waits for them, and re-layouts  104 us (15%)
  matrix products  94.3 us (13%)
  blocking collectives  37.7 us (5%)
  starting transfers between devices  24.7 us (4%)
  other arithmetic  14.7 us (2%)
    all_to_all x2, waiting for transfers between devices, per_device(): lax.all_to_all(lines, 'row', split_axis=0, concat_axis=0, tiled=True)  295 us
    all_to_all x2, waiting for transfers between devices, per_device(): lax.all_to_all(ytrans, 'col', split_axis=0, concat_axis=0, tiled=True)  126 us
    dot_general x2, matrix products, per_device(): jnp.einsum('dcsyf,sckyzm->dkmzf', y_table, gathered, precision=high)  55 us
    psum x1, blocking collectives, per_device(): coef = lax.psum(partial_value, ('row', 'col'))  37.7 us
    another operation x2, local copies, waits for them, and re-layouts, per_device(): gathered = with_layout_constraint(gathered, Layout((0, 1, 2, 3, 4)))  24.5 us
    dot_general x2, matrix products, per_device(): jnp.einsum('cxrk,ylx->rckyl', x_table[:, :, :, piece], flat, precision=high)  20.5 us
    concatenate x1, local copies, waits for them, and re-layouts, per_device(): whole = jnp.concatenate(outs, axis=2) if pieces > 1 else outs[0]  19.5 us
    dot_general x2, matrix products, per_device(): jnp.einsum('edszg,sdkmzf->gmkef', z_table, levels, precision=high)  16.5 us
  transfers between devices with their start and end apart: 4, of which 4 were waited for; matrix products, arithmetic and copies ran while one was open for 19% of the time, Pallas kernels for 0%

commit v1 on v0

--- a/solution.py
+++ b/solution.py
@@ -1,8 +1,12 @@
+import functools
 import math
 
 import jax
 import jax.numpy as jnp
+import numpy as np
 from jax import lax
+from jax.experimental import pallas as pl
+from jax.experimental.pallas import tpu as pltpu
 from jax.experimental.layout import Layout, with_layout_constraint
 from jax.sharding import PartitionSpec as P
 
@@ -43,7 +47,369 @@
     return jnp.stack([jnp.stack([cos, sin]), jnp.stack([-sin, cos])])
 
 
-def per_device(field, modes):
+MESH = pl.DeviceIdType.MESH
+LANES = 128
+SUB = 8
+
+
+def split(value):
+    top = value.astype(jnp.bfloat16)
+    rest = (value - top.astype(jnp.float32)).astype(jnp.bfloat16)
+    return top, rest
+
+
+def waves_of(length, scale):
+    j = np.arange(length)
+    coarse = 2.0 * np.pi * (np.arange(0, length, SUB)[:, None] * j[None, :] % length) / length
+    fine = 2.0 * np.pi * (np.arange(SUB)[:, None] * j[None, :] % length) / length
+    coarse = np.stack([np.cos(coarse), np.sin(coarse)]) * scale
+    fine = np.stack([np.cos(fine), np.sin(fine)])
+    return coarse.astype(np.float32), fine.astype(np.float32)
+
+
+def cmul(a, c, s):
+    re, im = a
+    if c == 1.0 and s == 0.0:
+        return a
+    if c == 0.0 and s == 1.0:
+        return im, -re
+    return re * c + im * s, im * c - re * s
+
+
+def fft(items):
+    n = len(items)
+    if n == 1:
+        return items
+    even, odd = fft(items[0::2]), fft(items[1::2])
+    out = [None] * n
+    for k in range(n // 2):
+        er, ei = even[k]
+        if 8 * k == n or 8 * k == 3 * n:
+            r, i = odd[k]
+            h = math.sqrt(0.5)
+            if 8 * k == n:
+                tr, ti = (r + i) * h, (i - r) * h
+            else:
+                tr, ti = (i - r) * h, (r + i) * (-h)
+        elif k == 0:
+            tr, ti = odd[k]
+        elif 4 * k == n:
+            tr, ti = odd[k][1], None
+        else:
+            angle = 2.0 * math.pi * k / n
+            tr, ti = cmul(odd[k], math.cos(angle), math.sin(angle))
+        if ti is None:
+            r = odd[k][0]
+            out[k] = (er + tr, ei - r)
+            out[k + n // 2] = (er - tr, ei + r)
+        else:
+            out[k] = (er + tr, ei + ti)
+            out[k + n // 2] = (er - tr, ei - ti)
+    return out
+
+
+class Plan:
+    def __init__(self, shape, rows, cols):
+        self.near, self.thick, self.members, self.width = shape
+        self.rows, self.cols = rows, cols
+        self.length = self.near * rows
+        self.depth = self.thick * cols
+        self.waves = self.width // 2 // rows
+        self.local_y = self.length // cols
+        self.parts = self.waves // SUB
+        self.pieces = self.members * self.parts
+        self.lanes = self.near * self.thick
+        self.tiles = self.lanes // LANES
+        self.slabs = rows * self.tiles
+
+    def fits(self):
+        def power(n):
+            return n > 1 and n & (n - 1) == 0
+
+        return (
+            power(self.rows)
+            and power(self.cols)
+            and self.waves % SUB == 0
+            and self.near * 2 == LANES
+            and self.local_y == LANES
+            and self.thick % 4 == 0
+            and self.rows % 2 == 0
+            and self.slabs == self.cols * self.thick
+            and self.depth == 64
+            and self.width % 256 == 0
+            and self.width == self.length
+        )
+
+
+def kernel(plan, factor, field, coarse, fine, out, A, B, D, xtab, ytab, lines, stage, row_send, row_recv, col_send, col_recv, in_sem, out_sem):
+    R, C, H, T = plan.rows, plan.cols, plan.parts, plan.tiles
+    near, thick = plan.near, plan.thick
+    row, col = lax.axis_index("row"), lax.axis_index("col")
+
+    def row_peer(k):
+        return (row ^ k, col)
+
+    def col_peer(k):
+        return (row, col ^ k)
+
+    row_order = list(range(R // 2, R)) + list(range(1, R // 2))
+    col_order = list(range(C // 2, C)) + list(range(1, C // 2))
+
+    def load(m, slot):
+        return [
+            pltpu.make_async_copy(field.at[:, z, m, :], lines.at[slot, pl.ds(z * near, near), :], in_sem.at[slot])
+            for z in range(thick)
+        ]
+
+    for copy in load(0, 0):
+        copy.start()
+
+    barrier = pltpu.get_barrier_semaphore()
+    for k in range(1, R):
+        pl.semaphore_signal(barrier, inc=1, device_id=row_peer(k), device_id_type=MESH)
+    for k in range(1, C):
+        pl.semaphore_signal(barrier, inc=1, device_id=col_peer(k), device_id_type=MESH)
+
+    fc, fs = fine[0], fine[1]
+
+    def x_rows(i, _):
+        h, r = i // R, i % R
+        a = r * H + h
+        uc, us = coarse[0, pl.ds(a, 1), :], coarse[1, pl.ds(a, 1), :]
+        block = jnp.concatenate([uc * fc - us * fs, -(us * fc + uc * fs)], axis=0)
+        top, rest = split(block)
+        at = pl.ds(pl.multiple_of(i * 2 * SUB, 2 * SUB), 2 * SUB)
+        xtab[0, at, :] = top
+        xtab[1, at, :] = rest
+        return 0
+
+    lax.fori_loop(0, H * R, x_rows, 0)
+
+    pl.semaphore_wait(barrier, R + C - 2)
+
+    def row_copy(p, k):
+        return pltpu.make_async_remote_copy(
+            A.at[p, pl.ds((row ^ k) * T, T)],
+            B.at[p, pl.ds(row * T, T)],
+            row_send.at[p],
+            row_recv.at[p, k],
+            device_id=row_peer(k),
+            device_id_type=MESH,
+        )
+
+    def row_wait(p, k):
+        return pltpu.make_async_remote_copy(
+            A.at[p, pl.ds((row ^ k) * T, T)],
+            B.at[p, pl.ds((row ^ k) * T, T)],
+            row_send.at[p],
+            row_recv.at[p, k],
+            device_id=row_peer(k),
+            device_id_type=MESH,
+        )
+
+    def col_copy(p, k):
+        return pltpu.make_async_remote_copy(
+            A.at[p, pl.ds((col ^ k) * thick, thick)],
+            D.at[p, pl.ds(col * thick, thick)],
+            col_send.at[p],
+            col_recv.at[p, k],
+            device_id=col_peer(k),
+            device_id_type=MESH,
+        )
+
+    def col_wait(p, k):
+        return pltpu.make_async_remote_copy(
+            A.at[p, pl.ds((col ^ k) * thick, thick)],
+            D.at[p, pl.ds((col ^ k) * thick, thick)],
+            col_send.at[p],
+            col_recv.at[p, k],
+            device_id=col_peer(k),
+            device_id_type=MESH,
+        )
+
+    def contract(a, b):
+        return lax.dot_general(a, b, (((1,), (1,)), ((), ())), preferred_element_type=jnp.float32)
+
+    chunk = 2 * LANES
+
+    for m in range(plan.members):
+        slot = m % 2
+        if m + 1 < plan.members:
+            for copy in load(m + 1, 1 - slot):
+                copy.start()
+        for copy in load(m, slot):
+            copy.wait()
+
+        def x_step(g, _):
+            at = pl.ds(pl.multiple_of(g * chunk, chunk), chunk)
+            top, rest = split(lines[slot, at, :])
+            got = contract(xtab[0], top) + (contract(xtab[0], rest) + contract(xtab[1], top))
+            for h in range(H):
+                for r in range(R):
+                    base = (h * R + r) * 2 * SUB
+                    for t in range(chunk // LANES):
+                        A[m * H + h, r * T + g * (chunk // LANES) + t] = got[base : base + 2 * SUB, t * LANES : (t + 1) * LANES]
+            return 0
+
+        lax.fori_loop(0, plan.lanes // chunk, x_step, 0)
+        for h in range(H):
+            p = m * H + h
+            mine = pl.ds(row * T, T)
+            B[p, mine] = A[p, mine]
+            for k in row_order:
+                row_copy(p, k).start()
+
+    length = plan.length
+
+    def y_rows(i, _):
+        blocks = []
+        for b in range(2):
+            a = 2 * i + b
+            uc, us = coarse[0, pl.ds(a, 1), :], coarse[1, pl.ds(a, 1), :]
+            blocks.append(jnp.concatenate([uc * fc - us * fs, us * fc + uc * fs], axis=1))
+        top, rest = split(jnp.concatenate(blocks, axis=0) * factor)
+        at = pl.ds(pl.multiple_of(i * 2 * SUB, 2 * SUB), 2 * SUB)
+        ytab[0, at, :] = top
+        ytab[1, at, :] = rest
+        return 0
+
+    lax.fori_loop(0, length // (2 * SUB), y_rows, 0)
+
+    low = lax.broadcasted_iota(jnp.int32, (T * 2 * SUB, LANES), 1) < near
+
+    def y_step(p):
+        evens, odds = [], []
+        for t in range(R // 2):
+            v0 = B[p, 2 * t * T : (2 * t + 1) * T].reshape(T * 2 * SUB, LANES)
+            v1 = B[p, (2 * t + 1) * T : (2 * t + 2) * T].reshape(T * 2 * SUB, LANES)
+            evens.append(jnp.where(low, v0, pltpu.roll(v1, near, 1)))
+            odds.append(jnp.where(low, pltpu.roll(v0, near, 1), v1))
+        left = jnp.concatenate([jnp.concatenate(evens, axis=1), jnp.concatenate(odds, axis=1)], axis=0)
+        top, rest = split(left)
+
+        def times(a, b):
+            return jnp.dot(a, b, preferred_element_type=jnp.float32)
+
+        for c in range(C):
+            at_c = slice(c * LANES, (c + 1) * LANES)
+            at_s = slice(length + c * LANES, length + (c + 1) * LANES)
+
+            def product(at):
+                return times(top, ytab[0, :, at]) + (times(rest, ytab[0, :, at]) + times(top, ytab[1, :, at]))
+
+            both = product(at_c).reshape(thick, 2, SUB, LANES), product(at_s).reshape(thick, 2, SUB, LANES)
+            re = both[0][:, 0] + both[1][:, 1]
+            im = both[0][:, 1] - both[1][:, 0]
+            A[p, c * thick : (c + 1) * thick, 0:SUB] = re
+            A[p, c * thick : (c + 1) * thick, SUB : 2 * SUB] = im
+
+    def slab(z):
+        inner = z % thick
+        return z // thick * thick + inner % 2 * (thick // 2) + inner // 2
+
+    eight = 8
+
+    def out_copy(p, slot):
+        m, h = p // H, p % H
+        q = pl.ds(pl.multiple_of(h * 2 * SUB, 2 * SUB), 2 * SUB)
+        return pltpu.make_async_copy(stage.at[slot], out.at[:, m, q, :], out_sem.at[slot])
+
+    def z_step(p, slot):
+        for z0 in range(eight):
+            items = []
+            for z1 in range(eight):
+                s = slab(z1 * eight + z0)
+                items.append((D[p, s, 0:SUB], D[p, s, SUB : 2 * SUB]))
+            for k0, value in enumerate(fft(items)):
+                angle = 2.0 * math.pi * z0 * k0 / 64
+                exact = z0 * k0 == 0
+                re, im = value if exact else cmul(value, math.cos(angle), math.sin(angle))
+                s = slab(k0 * eight + z0)
+                D[p, s, 0:SUB] = re
+                D[p, s, SUB : 2 * SUB] = im
+        for k0 in range(eight):
+            items = []
+            for z0 in range(eight):
+                s = slab(k0 * eight + z0)
+                items.append((D[p, s, 0:SUB], D[p, s, SUB : 2 * SUB]))
+            for k1, (re, im) in enumerate(fft(items)):
+                stage[slot, k0 + eight * k1, pl.ds(0, SUB, stride=2), :] = re
+                stage[slot, k0 + eight * k1, pl.ds(1, SUB, stride=2), :] = im
+
+    def finish(p):
+        slot = p % 2
+
+        @pl.when(p >= 2)
+        def _():
+            out_copy(p - 2, slot).wait()
+
+        for k in col_order:
+            col_wait(p, k).wait_recv()
+        z_step(p, slot)
+        out_copy(p, slot).start()
+
+    def step(p, _):
+        for k in row_order:
+            row_wait(p, k).wait_recv()
+        for k in row_order:
+            row_wait(p, k).wait_send()
+        y_step(p)
+        mine = pl.ds(col * thick, thick)
+        D[p, mine] = A[p, mine]
+        for k in col_order:
+            col_copy(p, k).start()
+
+        @pl.when(p >= 1)
+        def _():
+            finish(p - 1)
+
+        return 0
+
+    lax.fori_loop(0, plan.pieces, step, 0)
+    finish(plan.pieces - 1)
+    for p in (plan.pieces - 2, plan.pieces - 1):
+        out_copy(p, p % 2).wait()
+
+    def drain(p, _):
+        for k in col_order:
+            col_copy(p, k).wait_send()
+        return 0
+
+    lax.fori_loop(0, plan.pieces, drain, 0)
+
+
+def exchanged(plan, field, factor):
+    coarse, fine = waves_of(plan.length, 1.0)
+    block = (plan.pieces, plan.slabs, 2 * SUB, LANES)
+    return pl.pallas_call(
+        functools.partial(kernel, plan, factor),
+        out_shape=jax.ShapeDtypeStruct((plan.depth, plan.members, 2 * plan.waves, plan.local_y), jnp.float32),
+        in_specs=[
+            pl.BlockSpec(memory_space=pl.ANY),
+            pl.BlockSpec(memory_space=pltpu.VMEM),
+            pl.BlockSpec(memory_space=pltpu.VMEM),
+        ],
+        out_specs=pl.BlockSpec(memory_space=pl.ANY),
+        scratch_shapes=[
+            pltpu.VMEM(block, jnp.float32),
+            pltpu.VMEM(block, jnp.float32),
+            pltpu.VMEM(block, jnp.float32),
+            pltpu.VMEM((2, plan.width, plan.width), jnp.bfloat16),
+            pltpu.VMEM((2, plan.length, 2 * plan.length), jnp.bfloat16),
+            pltpu.VMEM((2, plan.lanes, plan.width), jnp.float32),
+            pltpu.VMEM((2, plan.depth, 2 * SUB, LANES), jnp.float32),
+            pltpu.SemaphoreType.DMA((plan.pieces,)),
+            pltpu.SemaphoreType.DMA((plan.pieces, plan.rows)),
+            pltpu.SemaphoreType.DMA((plan.pieces,)),
+            pltpu.SemaphoreType.DMA((plan.pieces, plan.cols)),
+            pltpu.SemaphoreType.DMA((2,)),
+            pltpu.SemaphoreType.DMA((2,)),
+        ],
+        compiler_params=pltpu.CompilerParams(collective_id=0, has_side_effects=True, vmem_limit_bytes=67043328),
+    )(field, jnp.asarray(coarse), jnp.asarray(fine))
+
+
+def general(field):
     members = field.shape[2]
     width = field.shape[3]
     rows, cols = lax.axis_size("row"), lax.axis_size("col")
@@ -74,6 +440,14 @@
     whole = jnp.concatenate(outs, axis=2) if pieces > 1 else outs[0]
     local_q = 2 * waves
     whole = whole.reshape(depth, members, local_q, local_y)
+    return whole
+
+
+def per_device(field, modes):
+    rows, cols = lax.axis_size("row"), lax.axis_size("col")
+    plan = Plan(field.shape, rows, cols)
+    members, depth, waves, local_y = plan.members, plan.depth, plan.waves, plan.local_y
+    whole = exchanged(plan, field, 1.0 / math.sqrt(NX * NY * NZ)) if plan.fits() else general(field)
     spectrum = jnp.transpose(whole, (0, 3, 1, 2))
     row_start = lax.axis_index("row") * waves
     col_start = lax.axis_index("col") * local_y

time: 705 us -> 455 us (0.65)
  waiting for transfers between devices: 422 us -> 0 us
  Pallas kernels: 0 us -> 381 us
  matrix products: 94.3 us -> 2.27 us
  local copies, waits for them, and re-layouts: 104 us -> 22 us
  starting transfers between devices: 24.7 us -> 0 us
  other arithmetic: 14.7 us -> 7.17 us
    all_to_all x4 -> x0, waiting for transfers between devices: 422 us -> none  [the longest x2 295 us: per_device(): lax.all_to_all(lines, 'row', split_axis=0, concat_axis=0, tiled=True)]
    pallas_call x0 -> x1, Pallas kernels: none -> 381 us  [exchanged(): pl.pallas_call(functools.partial(kernel, plan, factor), out_shape=jax.Sha...]
    dot_general x6 -> x0, matrix products: 92 us -> none  [the longest x2 55 us: per_device(): jnp.einsum('dcsyf,sckyzm->dkmzf', y_table, gathered, precision=high)]
    all_to_all x4 -> x0, starting transfers between devices: 24.7 us -> none  [the longest x2 12.8 us: per_device(): lax.all_to_all(lines, 'row', split_axis=0, concat_axis=0, tiled=True)]
    another operation x2 -> x0, local copies, waits for them, and re-layouts: 24.5 us -> none  [per_device(): gathered = with_layout_constraint(gathered, Layout((0, 1, 2, 3, 4)))]
    concatenate x1 -> x0, local copies, waits for them, and re-layouts: 19.5 us -> none  [per_device(): whole = jnp.concatenate(outs, axis=2) if pieces > 1 else outs[0]]
    reshape x2 -> x0, local copies, waits for them, and re-layouts: 16.3 us -> none  [per_device(): ytrans = ytrans.reshape(2, part, members, thick, cols, local_y)]
    dot_general x4 -> x0, local copies, waits for them, and re-layouts: 14.7 us -> none  [the longest x2 11.8 us: per_device(): jnp.einsum('cxrk,ylx->rckyl', x_table[:, :, :, piece], flat, precision=high)]
  transfers between devices with their start and end apart: 4 -> 0, of which waited for: 4 -> 0; matrix products, arithmetic and copies ran while one was open for 19% -> 0% of each run, Pallas kernels for 0% -> 0%
where the time goes in v1:
time: 455 us
  Pallas kernels  381 us (84%)
  blocking collectives  41.3 us (9%)
  local copies, waits for them, and re-layouts  22 us (5%)
  other arithmetic  7.17 us (2%)
    pallas_call x1, Pallas kernels, exchanged(): pl.pallas_call(functools.partial(kernel, plan, factor), out_shape=jax.Sha...  381 us
    psum x1, blocking collectives, per_device(): coef = lax.psum(partial_value, ('row', 'col'))  41.3 us
    unnamed x10, local copies, waits for them, and re-layouts  12 us
    gather x1, local copies, waits for them, and re-layouts, per_device(): picked = tall[modes[2], :, wave]  9.63 us

profile of v1, /device:TPU:0, one launch (start us, length us, event | category | flops | bytes accessed | tf_op | source)
XLA Modules:
  0.0 454.7 jit_solution(845331596985951866)
XLA Ops:
  0.6 0.7 and_reduce_fusion
  1.3 1.3 fusion.8
  2.7 0.8 slice_convert_fusion
  3.5 0.6 pad_maximum_fusion.2
  4.1 0.6 pad_maximum_fusion
  4.7 0.8 fusion.1
  5.4 381.2 %shard_map.59 = f32[64,8,64,128]{3,2,1,0:T(8,128)} custom-call(f32[64,16,8,512]{3,2,1,0:T(8,128)} %field.1, f32[2,64,512]{2,1,0:T(8,128)} %constant.46.clone.coarse, f32[2,8,512]{2,1,0:T(8,128)} %constant.47.clone.fine), custom_call_target="tpu_custom_call" | custom-call | tf_op jit(solution)/shard_map/pallas_call | solution.py:384
  386.6 0.0 copy-start
  386.6 9.6 %gather_fusion = f32[256,8,2,128]{3,2,1,0:T(2,128)S(1)} fusion(f32[64,8,32,2,128]{4,3,2,1,0:T(2,128)} %bitcast.13, s32[256]{0:T(256)} %bitcast.15), kind=kCustom, calls=%fused_computation | custom fusion | bytes 4196352 | tf_op jit(solution)/shard_map/gather | solution.py:461
  396.2 0.0 copy-done
  396.3 0.0 copy-start.1
  396.3 0.0 copy-start.2
  396.3 0.0 copy-start.3
  396.3 2.4 select_reduce_fusion
  398.7 0.4 copy.6
  399.0 41.3 %psum.7 = f32[8,512]{1,0:T(8,128)S(1)} all-reduce(f32[8,512]{1,0:T(8,128)S(1)} %bitcast.18), channel_id=1, replica_groups=mesh['row'=8,'col'=4] {'row','col'}, use_global_device_ids=true, to_apply=%region_1.2 | all-reduce | flops 4096 | bytes 32768 | tf_op jit(solution)/shard_map/psum | solution.py:465
  440.4 0.0 copy-done.1
  440.4 0.0 copy-done.2
  440.4 0.0 copy-done.3
  440.4 2.3 fusion
  442.7 12.0 %copy.9 = f32[64,128,8,64]{1,3,2,0:T(8,128)} copy(f32[64,128,8,64]{1,3,2,0:T(8,128)} %bitcast.14) | data formatting | bytes 33554432
  (6 shorter events, 0.1 us)
Async XLA Ops:
  386.6 9.7 %copy-start = (pred[256,128]{1,0:T(8,128)(4,1)S(1)}, pred[256,128]{1,0:T(8,128)(4,1)}, u32[]{:S(2)}) copy-start(pred[256,128]{1,0:T(8,128)(4,1)} %fusion.1) | copy-start | bytes 98308
  396.3 44.2 %copy-start.1 = (f32[512]{0:T(512)S(1)}, f32[512]{0:T(512)}, u32[]{:S(2)}) copy-start(f32[512]{0:T(512)} %get-tuple-element.7) | copy-start | bytes 6148
  396.3 44.2 %copy-start.2 = (f32[512]{0:T(512)S(1)}, f32[512]{0:T(512)}, u32[]{:S(2)}) copy-start(f32[512]{0:T(512)} %get-tuple-element.8) | copy-start | bytes 6148
  396.3 44.2 %copy-start.3 = (f32[512]{0:T(512)S(1)}, f32[512]{0:T(512)}, u32[]{:S(2)}) copy-start(f32[512]{0:T(512)} %pad_maximum_fusion.2) | copy-start | bytes 6148

commit v2 on v1

--- a/solution.py
+++ b/solution.py
@@ -49,6 +49,7 @@
 
 MESH = pl.DeviceIdType.MESH
 LANES = 128
+LIMIT = 49000000
 SUB = 8
 
 
@@ -138,10 +139,16 @@
             and self.depth == 64
             and self.width % 256 == 0
             and self.width == self.length
-        )
-
-
-def kernel(plan, factor, field, coarse, fine, out, A, B, D, xtab, ytab, lines, stage, row_send, row_recv, col_send, col_recv, in_sem, out_sem):
+            and power(self.length)
+            and self.members == SUB
+        )
+
+
+def kernel(
+    plan, factor, field, modes, coarse, fine, D, localized,
+    A, B, xtab, ytab, ptab, lines, mid, part, subtotal, col_parts, row_parts,
+    row_send, row_recv, col_send, col_recv, in_sem, sum_send, sum_col, sum_row,
+):
     R, C, H, T = plan.rows, plan.cols, plan.parts, plan.tiles
     near, thick = plan.near, plan.thick
     row, col = lax.axis_index("row"), lax.axis_index("col")
@@ -258,6 +265,80 @@
             B[p, mine] = A[p, mine]
             for k in row_order:
                 row_copy(p, k).start()
+
+    count = modes.shape[1]
+    pick_x, pick_y, pick_z = modes[0:1, :], modes[1:2, :], modes[2:3, :]
+
+    def phase_rows(t, _):
+        cell = t * LANES + lax.broadcasted_iota(jnp.int32, (LANES, count), 0)
+        y = row * near + cell % near
+        z = col * thick + cell // near
+        turns = (pick_y * y + (plan.length // plan.depth) * pick_z * z) % plan.length
+        half = (turns - plan.length // 2).astype(jnp.float32) * (math.pi / plan.length)
+        square = half * half
+        sine, cosine = 1.0, 1.0
+        for n in range(6, 0, -1):
+            sine = 1.0 - square * sine * (1.0 / (2 * n * (2 * n + 1)))
+        for n in range(7, 0, -1):
+            cosine = 1.0 - square * cosine * (1.0 / (2 * n * (2 * n - 1)))
+        sine = half * sine
+        top, rest = split(jnp.concatenate([2.0 * sine * sine - 1.0, -2.0 * sine * cosine], axis=1))
+        at = pl.ds(pl.multiple_of(t * LANES, LANES), LANES)
+        ptab[0, at, :] = top
+        ptab[1, at, :] = rest
+        return 0
+
+    lax.fori_loop(0, plan.lanes // LANES, phase_rows, 0)
+    part[...] = jnp.zeros_like(part)
+    owner = lax.broadcasted_iota(jnp.int32, (R, SUB, count), 0)
+    inner = lax.broadcasted_iota(jnp.int32, (R, SUB, count), 1)
+
+    def part_step(p, _):
+        m, h = p // H, p % H
+        cells = jnp.concatenate(
+            [jnp.concatenate([A[p, r * T + t] for t in range(T)], axis=1) for r in range(R)], axis=0
+        )
+        top, rest = split(cells)
+
+        def times(a, b):
+            return jnp.dot(a, b, preferred_element_type=jnp.float32)
+
+        got = times(top, ptab[0]) + (times(rest, ptab[0]) + times(top, ptab[1]))
+        got = got.reshape(R, 2, SUB, 2 * count)
+        re = got[:, 0, :, :count] + got[:, 1, :, count:]
+        im = got[:, 1, :, :count] - got[:, 0, :, count:]
+        hit = owner * plan.waves + h * SUB + inner == pick_x.reshape(1, 1, count)
+        for c, value in enumerate((re, im)):
+            found = jnp.sum(jnp.where(hit, value, 0.0), axis=(0, 1)).reshape(1, count)
+            at = slice(c * count, (c + 1) * count)
+            part[pl.ds(m, 1), at] = part[pl.ds(m, 1), at] + found
+        return 0
+
+    lax.fori_loop(0, plan.pieces, part_step, 0)
+    col_parts[col] = part[...]
+
+    def col_sum(k):
+        return pltpu.make_async_remote_copy(
+            part, col_parts.at[col], sum_send.at[0], sum_col.at[k], device_id=col_peer(k), device_id_type=MESH
+        )
+
+    def col_sum_wait(k):
+        return pltpu.make_async_remote_copy(
+            part, col_parts.at[col ^ k], sum_send.at[0], sum_col.at[k], device_id=col_peer(k), device_id_type=MESH
+        )
+
+    def row_sum(k):
+        return pltpu.make_async_remote_copy(
+            subtotal, row_parts.at[row], sum_send.at[1], sum_row.at[k], device_id=row_peer(k), device_id_type=MESH
+        )
+
+    def row_sum_wait(k):
+        return pltpu.make_async_remote_copy(
+            subtotal, row_parts.at[row ^ k], sum_send.at[1], sum_row.at[k], device_id=row_peer(k), device_id_type=MESH
+        )
+
+    for k in col_order:
+        col_sum(k).start()
 
     length = plan.length
 
@@ -275,6 +356,16 @@
 
     lax.fori_loop(0, length // (2 * SUB), y_rows, 0)
 
+    for k in col_order:
+        col_sum_wait(k).wait_recv()
+    total = col_parts[0]
+    for c in range(1, C):
+        total = total + col_parts[c]
+    subtotal[...] = total
+    row_parts[row] = total
+    for k in row_order:
+        row_sum(k).start()
+
     low = lax.broadcasted_iota(jnp.int32, (T * 2 * SUB, LANES), 1) < near
 
     def y_step(p):
@@ -309,44 +400,30 @@
 
     eight = 8
 
-    def out_copy(p, slot):
-        m, h = p // H, p % H
-        q = pl.ds(pl.multiple_of(h * 2 * SUB, 2 * SUB), 2 * SUB)
-        return pltpu.make_async_copy(stage.at[slot], out.at[:, m, q, :], out_sem.at[slot])
-
-    def z_step(p, slot):
+    def z_step(p):
         for z0 in range(eight):
             items = []
             for z1 in range(eight):
-                s = slab(z1 * eight + z0)
-                items.append((D[p, s, 0:SUB], D[p, s, SUB : 2 * SUB]))
+                at = slab(z1 * eight + z0)
+                items.append((D[p, at, 0:SUB], D[p, at, SUB : 2 * SUB]))
             for k0, value in enumerate(fft(items)):
                 angle = 2.0 * math.pi * z0 * k0 / 64
-                exact = z0 * k0 == 0
-                re, im = value if exact else cmul(value, math.cos(angle), math.sin(angle))
-                s = slab(k0 * eight + z0)
-                D[p, s, 0:SUB] = re
-                D[p, s, SUB : 2 * SUB] = im
+                re, im = value if z0 * k0 == 0 else cmul(value, math.cos(angle), math.sin(angle))
+                mid[k0 * eight + z0, 0:SUB] = re
+                mid[k0 * eight + z0, SUB : 2 * SUB] = im
         for k0 in range(eight):
             items = []
             for z0 in range(eight):
-                s = slab(k0 * eight + z0)
-                items.append((D[p, s, 0:SUB], D[p, s, SUB : 2 * SUB]))
+                at = k0 * eight + z0
+                items.append((mid[at, 0:SUB], mid[at, SUB : 2 * SUB]))
             for k1, (re, im) in enumerate(fft(items)):
-                stage[slot, k0 + eight * k1, pl.ds(0, SUB, stride=2), :] = re
-                stage[slot, k0 + eight * k1, pl.ds(1, SUB, stride=2), :] = im
+                D[p, k0 + eight * k1, pl.ds(0, SUB, stride=2), :] = re
+                D[p, k0 + eight * k1, pl.ds(1, SUB, stride=2), :] = im
 
     def finish(p):
-        slot = p % 2
-
-        @pl.when(p >= 2)
-        def _():
-            out_copy(p - 2, slot).wait()
-
         for k in col_order:
             col_wait(p, k).wait_recv()
-        z_step(p, slot)
-        out_copy(p, slot).start()
+        z_step(p)
 
     def step(p, _):
         for k in row_order:
@@ -365,48 +442,119 @@
 
         return 0
 
+    def localize():
+        for k in row_order:
+            row_sum_wait(k).wait_recv()
+        total = row_parts[0]
+        for r in range(1, R):
+            total = total + row_parts[r]
+        coef = total * factor
+        anomaly = coef - jnp.sum(coef, axis=0, keepdims=True) / plan.members
+        columns = 2 * count
+
+        def signed(wave, size):
+            return jnp.where(wave < size // 2, wave, wave - size).astype(jnp.float32)
+
+        places = [pick_x.astype(jnp.float32), signed(pick_y, plan.length), signed(pick_z, plan.depth)]
+        places = [jnp.concatenate([place, place], axis=1) for place in places]
+        squares = places[0] * places[0] + places[1] * places[1] + places[2] * places[2]
+        ones = jnp.ones_like(squares)
+        nothing = jnp.zeros((LANES - 5, columns), jnp.float32)
+        left = jnp.concatenate(places + [squares, ones, nothing], axis=0)
+        right = jnp.concatenate([-2.0 * place for place in places] + [ones, squares, nothing], axis=0)
+        padded = jnp.concatenate([anomaly, jnp.zeros((LANES - plan.members, columns), jnp.float32)], axis=0)
+        left, turned = jnp.transpose(left), jnp.transpose(padded)
+
+        def times(a, b):
+            return jnp.dot(a, b, precision=highest, preferred_element_type=jnp.float32)
+
+        for i in range(0, columns, LANES):
+            cov = times(turned[i : i + LANES], padded) / (plan.members - 1)
+            dist = times(left[i : i + LANES], right)
+            localized[i : i + LANES, :] = cov * jnp.exp(-dist / (2.0 * REACH * REACH))
+
     lax.fori_loop(0, plan.pieces, step, 0)
+    localize()
     finish(plan.pieces - 1)
-    for p in (plan.pieces - 2, plan.pieces - 1):
-        out_copy(p, p % 2).wait()
-
     def drain(p, _):
         for k in col_order:
             col_copy(p, k).wait_send()
         return 0
 
     lax.fori_loop(0, plan.pieces, drain, 0)
-
-
-def exchanged(plan, field, factor):
+    for k in col_order:
+        col_sum(k).wait_send()
+    for k in row_order:
+        row_sum(k).wait_send()
+
+
+def exchanged(plan, field, modes, factor):
     coarse, fine = waves_of(plan.length, 1.0)
+    count = modes.shape[1]
+    sums = (plan.members, 2 * count)
     block = (plan.pieces, plan.slabs, 2 * SUB, LANES)
     return pl.pallas_call(
         functools.partial(kernel, plan, factor),
-        out_shape=jax.ShapeDtypeStruct((plan.depth, plan.members, 2 * plan.waves, plan.local_y), jnp.float32),
+        out_shape=(
+            pltpu.VMEM(block, jnp.float32),
+            pltpu.VMEM((2 * count, 2 * count), jnp.float32),
+        ),
         in_specs=[
             pl.BlockSpec(memory_space=pl.ANY),
             pl.BlockSpec(memory_space=pltpu.VMEM),
             pl.BlockSpec(memory_space=pltpu.VMEM),
+            pl.BlockSpec(memory_space=pltpu.VMEM),
         ],
-        out_specs=pl.BlockSpec(memory_space=pl.ANY),
+        out_specs=(pl.BlockSpec(memory_space=pltpu.VMEM), pl.BlockSpec(memory_space=pltpu.VMEM)),
         scratch_shapes=[
-            pltpu.VMEM(block, jnp.float32),
             pltpu.VMEM(block, jnp.float32),
             pltpu.VMEM(block, jnp.float32),
             pltpu.VMEM((2, plan.width, plan.width), jnp.bfloat16),
             pltpu.VMEM((2, plan.length, 2 * plan.length), jnp.bfloat16),
+            pltpu.VMEM((2, plan.lanes, 2 * count), jnp.bfloat16),
             pltpu.VMEM((2, plan.lanes, plan.width), jnp.float32),
-            pltpu.VMEM((2, plan.depth, 2 * SUB, LANES), jnp.float32),
+            pltpu.VMEM((plan.depth, 2 * SUB, LANES), jnp.float32),
+            pltpu.VMEM(sums, jnp.float32),
+            pltpu.VMEM(sums, jnp.float32),
+            pltpu.VMEM((plan.cols,) + sums, jnp.float32),
+            pltpu.VMEM((plan.rows,) + sums, jnp.float32),
             pltpu.SemaphoreType.DMA((plan.pieces,)),
             pltpu.SemaphoreType.DMA((plan.pieces, plan.rows)),
             pltpu.SemaphoreType.DMA((plan.pieces,)),
             pltpu.SemaphoreType.DMA((plan.pieces, plan.cols)),
             pltpu.SemaphoreType.DMA((2,)),
             pltpu.SemaphoreType.DMA((2,)),
+            pltpu.SemaphoreType.DMA((plan.cols,)),
+            pltpu.SemaphoreType.DMA((plan.rows,)),
         ],
-        compiler_params=pltpu.CompilerParams(collective_id=0, has_side_effects=True, vmem_limit_bytes=67043328),
-    )(field, jnp.asarray(coarse), jnp.asarray(fine))
+        compiler_params=pltpu.CompilerParams(collective_id=0, has_side_effects=True, vmem_limit_bytes=LIMIT),
+    )(field, modes, jnp.asarray(coarse), jnp.asarray(fine))
+
+
+def settle(plan, piled, square, whole, localized, sems):
+    H = plan.parts
+    copies = [pltpu.make_async_copy(square, localized, sems.at[plan.pieces])]
+    for p in range(plan.pieces):
+        m, h = p // H, p % H
+        copies.append(pltpu.make_async_copy(piled.at[p], whole.at[:, m, pl.ds(h * 2 * SUB, 2 * SUB), :], sems.at[p]))
+    for copy in copies:
+        copy.start()
+    for copy in copies:
+        copy.wait()
+
+
+def settled(plan, piled, square):
+    return pl.pallas_call(
+        functools.partial(settle, plan),
+        out_shape=(
+            jax.ShapeDtypeStruct((plan.depth, plan.members, 2 * plan.waves, plan.local_y), jnp.float32),
+            jax.ShapeDtypeStruct(square.shape, jnp.float32),
+        ),
+        in_specs=[pl.BlockSpec(memory_space=pltpu.VMEM), pl.BlockSpec(memory_space=pltpu.VMEM)],
+        out_specs=(pl.BlockSpec(memory_space=pl.ANY), pl.BlockSpec(memory_space=pl.ANY)),
+        scratch_shapes=[pltpu.SemaphoreType.DMA((plan.pieces + 1,))],
+        compiler_params=pltpu.CompilerParams(vmem_limit_bytes=1 << 20),
+    )(pltpu.with_memory_space_constraint(piled, pltpu.VMEM), pltpu.with_memory_space_constraint(square, pltpu.VMEM))
 
 
 def general(field):
@@ -443,12 +591,10 @@
     return whole
 
 
-def per_device(field, modes):
+def general_localized(whole, modes):
     rows, cols = lax.axis_size("row"), lax.axis_size("col")
-    plan = Plan(field.shape, rows, cols)
-    members, depth, waves, local_y = plan.members, plan.depth, plan.waves, plan.local_y
-    whole = exchanged(plan, field, 1.0 / math.sqrt(NX * NY * NZ)) if plan.fits() else general(field)
-    spectrum = jnp.transpose(whole, (0, 3, 1, 2))
+    depth, members, local_q, local_y = whole.shape
+    waves = local_q // 2
     row_start = lax.axis_index("row") * waves
     col_start = lax.axis_index("col") * local_y
     wave = modes[0] - row_start
@@ -466,7 +612,18 @@
     anomaly = coef - jnp.mean(coef, axis=0, keepdims=True)
     cov = jnp.dot(anomaly.T, anomaly, precision=highest) / (members - 1)
     localized = cov * taper_of(modes, NY, NZ, REACH)
-    return (spectrum, localized)
+    return localized
+
+
+def per_device(field, modes):
+    plan = Plan(field.shape, lax.axis_size("row"), lax.axis_size("col"))
+    factor = 1.0 / math.sqrt(NX * NY * NZ)
+    if plan.fits() and modes.shape[1] % LANES == 0:
+        whole, localized = settled(plan, *exchanged(plan, field, modes, factor))
+    else:
+        whole = general(field)
+        localized = general_localized(whole, modes)
+    return (jnp.transpose(whole, (0, 3, 1, 2)), localized)
 
 
 def solution(mesh):

time: 455 us -> 391 us (0.86)
  blocking collectives: 41.3 us -> 0 us
  local copies, waits for them, and re-layouts: 22 us -> 0 us
  other arithmetic: 7.17 us -> 0 us
  Pallas kernels: 381 us -> 388 us
    psum x1 -> x0, blocking collectives: 41.3 us -> none  [per_device(): coef = lax.psum(partial_value, ('row', 'col'))]
    unnamed x10 -> x0, local copies, waits for them, and re-layouts: 12 us -> none
    gather x1 -> x0, local copies, waits for them, and re-layouts: 9.63 us -> none  [per_device(): picked = tall[modes[2], :, wave]]
    pallas_call x1 -> x2, Pallas kernels: 381 us -> 388 us  [the longest x1 382 us: exchanged(): pl.pallas_call(functools.partial(kernel, plan, factor), out_shape=(pltpu....]
where the time goes in v2:
time: 391 us; the launch traced here: 389 us
  Pallas kernels  388 us (99%)
    pallas_call x1, Pallas kernels, exchanged(): pl.pallas_call(functools.partial(kernel, plan, factor), out_shape=(pltpu....  382 us

profile of v2, /device:TPU:0, one launch (start us, length us, event | category | flops | bytes accessed | tf_op | source)
XLA Modules:
  0.0 388.7 jit_solution(5785220569093866251)
XLA Ops:
  0.6 381.7 %shard_map.59 = (f32[32,64,16,128]{3,2,1,0:T(8,128)S(1)}, f32[512,512]{1,0:T(8,128)S(1)}) custom-call(f32[64,16,8,512]{3,2,1,0:T(8,128)} %field.1, s32[3,256]{1,0:T(4,128)} %modes.1, f32[2,64,512]{2,1,0:T(8,128)} %constant.4.clone.coarse, f32[2,8,512]{2,1,0:T(8,128)} %constant.5.clone.fine), custom_call_target="tpu_custom_call" | custom-call | tf_op jit(solution)/shard_map/pallas_call | solution.py:496
  382.3 6.4 %shard_map.60 = (f32[64,8,64,128]{3,2,1,0:T(8,128)}, f32[512,512]{1,0:T(8,128)}) custom-call(f32[32,64,16,128]{3,2,1,0:T(8,128)S(1)} %get-tuple-element.6.piled, f32[512,512]{1,0:T(8,128)S(1)} %get-tuple-element.7.square), custom_call_target="tpu_custom_call" | custom-call | tf_op jit(solution)/shard_map/pallas_call | solution.py:547

commit v3 on v2

--- a/solution.py
+++ b/solution.py
@@ -122,6 +122,7 @@
         self.lanes = self.near * self.thick
         self.tiles = self.lanes // LANES
         self.slabs = rows * self.tiles
+        self.groups = 4
 
     def fits(self):
         def power(n):
@@ -133,7 +134,8 @@
             and self.waves % SUB == 0
             and self.near * 2 == LANES
             and self.local_y == LANES
-            and self.thick % 4 == 0
+            and self.thick % (2 * self.groups) == 0
+            and self.members >= 3
             and self.rows % 2 == 0
             and self.slabs == self.cols * self.thick
             and self.depth == 64
@@ -145,12 +147,14 @@
 
 
 def kernel(
-    plan, factor, field, modes, coarse, fine, D, localized,
-    A, B, xtab, ytab, ptab, lines, mid, part, subtotal, col_parts, row_parts,
-    row_send, row_recv, col_send, col_recv, in_sem, sum_send, sum_col, sum_row,
+    plan, factor, field, modes_in, coarse_in, fine_in, D, localized,
+    A, B, last, xtab, ytab, ptab, lines, mid, modes, coarse, fine, part, subtotal, col_parts, row_parts,
+    row_send, row_recv, col_send, col_recv, in_sem, table_sem, sum_send, sum_col, sum_row,
 ):
     R, C, H, T = plan.rows, plan.cols, plan.parts, plan.tiles
-    near, thick = plan.near, plan.thick
+    near, thick, groups = plan.near, plan.thick, plan.groups
+    ply, deep = T // groups, thick // groups
+    final = plan.pieces - 1
     row, col = lax.axis_index("row"), lax.axis_index("col")
 
     def row_peer(k):
@@ -162,20 +166,27 @@
     row_order = list(range(R // 2, R)) + list(range(1, R // 2))
     col_order = list(range(C // 2, C)) + list(range(1, C // 2))
 
-    def load(m, slot):
-        return [
-            pltpu.make_async_copy(field.at[:, z, m, :], lines.at[slot, pl.ds(z * near, near), :], in_sem.at[slot])
-            for z in range(thick)
-        ]
-
-    for copy in load(0, 0):
+    def load(m, z, sem):
+        at = pl.ds(pl.multiple_of(z * near, near), near)
+        return pltpu.make_async_copy(field.at[:, z, m, :], lines.at[m % 2, at, :], in_sem.at[sem])
+
+    tables = [
+        pltpu.make_async_copy(coarse_in, coarse, table_sem.at[0]),
+        pltpu.make_async_copy(fine_in, fine, table_sem.at[1]),
+        pltpu.make_async_copy(modes_in, modes, table_sem.at[2]),
+    ]
+    for copy in tables:
         copy.start()
+    for z in range(thick):
+        load(0, z, z // deep).start()
 
     barrier = pltpu.get_barrier_semaphore()
     for k in range(1, R):
         pl.semaphore_signal(barrier, inc=1, device_id=row_peer(k), device_id_type=MESH)
     for k in range(1, C):
         pl.semaphore_signal(barrier, inc=1, device_id=col_peer(k), device_id_type=MESH)
+    for copy in tables:
+        copy.wait()
 
     fc, fs = fine[0], fine[1]
 
@@ -194,77 +205,94 @@
 
     pl.semaphore_wait(barrier, R + C - 2)
 
-    def row_copy(p, k):
+    def row_copy(src, dst, unit, k):
         return pltpu.make_async_remote_copy(
-            A.at[p, pl.ds((row ^ k) * T, T)],
-            B.at[p, pl.ds(row * T, T)],
-            row_send.at[p],
-            row_recv.at[p, k],
-            device_id=row_peer(k),
-            device_id_type=MESH,
-        )
-
-    def row_wait(p, k):
+            src, dst, row_send.at[unit], row_recv.at[unit, k], device_id=row_peer(k), device_id_type=MESH
+        )
+
+    def row_part(p, k, unit, first=0, size=T):
+        return row_copy(
+            A.at[p, pl.ds((row ^ k) * T + first, size)], B.at[p, pl.ds(row * T + first, size)], unit, k
+        )
+
+    def row_wait(p, k, unit, first=0, size=T):
+        return row_copy(
+            A.at[p, pl.ds((row ^ k) * T + first, size)], B.at[p, pl.ds((row ^ k) * T + first, size)], unit, k
+        )
+
+    def col_copy(src, dst, unit, k):
         return pltpu.make_async_remote_copy(
-            A.at[p, pl.ds((row ^ k) * T, T)],
-            B.at[p, pl.ds((row ^ k) * T, T)],
-            row_send.at[p],
-            row_recv.at[p, k],
-            device_id=row_peer(k),
-            device_id_type=MESH,
-        )
-
-    def col_copy(p, k):
-        return pltpu.make_async_remote_copy(
-            A.at[p, pl.ds((col ^ k) * thick, thick)],
-            D.at[p, pl.ds(col * thick, thick)],
-            col_send.at[p],
-            col_recv.at[p, k],
-            device_id=col_peer(k),
-            device_id_type=MESH,
-        )
-
-    def col_wait(p, k):
-        return pltpu.make_async_remote_copy(
-            A.at[p, pl.ds((col ^ k) * thick, thick)],
-            D.at[p, pl.ds((col ^ k) * thick, thick)],
-            col_send.at[p],
-            col_recv.at[p, k],
-            device_id=col_peer(k),
-            device_id_type=MESH,
+            src, dst, col_send.at[unit], col_recv.at[unit, k], device_id=col_peer(k), device_id_type=MESH
+        )
+
+    def col_part(out, p, k, unit, first=0, size=thick):
+        return col_copy(
+            out.at[pl.ds((col ^ k) * thick + first, size)], D.at[p, pl.ds(col * thick + first, size)], unit, k
+        )
+
+    def col_wait(out, p, k, unit, first=0, size=thick):
+        return col_copy(
+            out.at[pl.ds((col ^ k) * thick + first, size)], D.at[p, pl.ds((col ^ k) * thick + first, size)], unit, k
         )
 
     def contract(a, b):
         return lax.dot_general(a, b, (((1,), (1,)), ((), ())), preferred_element_type=jnp.float32)
 
-    chunk = 2 * LANES
-
-    for m in range(plan.members):
-        slot = m % 2
+    chunk = ply * LANES
+
+    def x_step(m, g):
+        at = pl.ds(pl.multiple_of(g * chunk, chunk), chunk)
+        top, rest = split(lines[m % 2, at, :])
+        got = contract(xtab[0], top) + (contract(xtab[0], rest) + contract(xtab[1], top))
+        for h in range(H):
+            for r in range(R):
+                base = (h * R + r) * 2 * SUB
+                for t in range(ply):
+                    A[m * H + h, r * T + g * ply + t] = got[base : base + 2 * SUB, t * LANES : (t + 1) * LANES]
+
+    mine = pl.ds(row * T, T)
+
+    def x_first(g, _):
+        for z in range(deep):
+            load(0, g * deep + z, g).wait()
+        x_step(0, g)
+        for k in row_order:
+            row_copy(
+                A.at[pl.ds(0, H), pl.ds((row ^ k) * T + g * ply, ply)],
+                B.at[pl.ds(0, H), pl.ds(row * T + g * ply, ply)],
+                0,
+                k,
+            ).start()
+        return 0
+
+    lax.fori_loop(0, groups, x_first, 0)
+    for z in range(thick):
+        load(1, z, groups + 1).start()
+    for h in range(H):
+        B[h, mine] = A[h, mine]
+
+    for m in range(1, plan.members):
         if m + 1 < plan.members:
-            for copy in load(m + 1, 1 - slot):
-                copy.start()
-        for copy in load(m, slot):
-            copy.wait()
-
-        def x_step(g, _):
-            at = pl.ds(pl.multiple_of(g * chunk, chunk), chunk)
-            top, rest = split(lines[slot, at, :])
-            got = contract(xtab[0], top) + (contract(xtab[0], rest) + contract(xtab[1], top))
-            for h in range(H):
-                for r in range(R):
-                    base = (h * R + r) * 2 * SUB
-                    for t in range(chunk // LANES):
-                        A[m * H + h, r * T + g * (chunk // LANES) + t] = got[base : base + 2 * SUB, t * LANES : (t + 1) * LANES]
+            for z in range(thick):
+                load(m + 1, z, groups + (m + 1) % 2).start()
+        for z in range(thick):
+            load(m, z, groups + m % 2).wait()
+
+        def x_more(g, _):
+            x_step(m, g)
             return 0
 
-        lax.fori_loop(0, plan.lanes // chunk, x_step, 0)
+        lax.fori_loop(0, groups, x_more, 0)
         for h in range(H):
             p = m * H + h
-            mine = pl.ds(row * T, T)
             B[p, mine] = A[p, mine]
-            for k in row_order:
-                row_copy(p, k).start()
+            if p < final:
+                for k in row_order:
+                    row_part(p, k, p).start()
+            else:
+                for g in range(groups):
+                    for k in row_order:
+                        row_part(final, k, final + g, g * ply, ply).start()
 
     count = modes.shape[1]
     pick_x, pick_y, pick_z = modes[0:1, :], modes[1:2, :], modes[2:3, :]
@@ -347,7 +375,12 @@
         for b in range(2):
             a = 2 * i + b
             uc, us = coarse[0, pl.ds(a, 1), :], coarse[1, pl.ds(a, 1), :]
-            blocks.append(jnp.concatenate([uc * fc - us * fs, us * fc + uc * fs], axis=1))
+            cosine, sine = uc * fc - us * fs, us * fc + uc * fs
+            halves = []
+            for c in range(C):
+                at = slice(c * LANES, (c + 1) * LANES)
+                halves += [cosine[:, at], sine[:, at]]
+            blocks.append(jnp.concatenate(halves, axis=1))
         top, rest = split(jnp.concatenate(blocks, axis=0) * factor)
         at = pl.ds(pl.multiple_of(i * 2 * SUB, 2 * SUB), 2 * SUB)
         ytab[0, at, :] = top
@@ -366,13 +399,13 @@
     for k in row_order:
         row_sum(k).start()
 
-    low = lax.broadcasted_iota(jnp.int32, (T * 2 * SUB, LANES), 1) < near
-
-    def y_step(p):
+
+    def y_step(p, out, unit, first, size):
+        low = lax.broadcasted_iota(jnp.int32, (size * 2 * SUB, LANES), 1) < near
         evens, odds = [], []
         for t in range(R // 2):
-            v0 = B[p, 2 * t * T : (2 * t + 1) * T].reshape(T * 2 * SUB, LANES)
-            v1 = B[p, (2 * t + 1) * T : (2 * t + 2) * T].reshape(T * 2 * SUB, LANES)
+            v0 = B[p, 2 * t * T + first : 2 * t * T + first + size].reshape(size * 2 * SUB, LANES)
+            v1 = B[p, (2 * t + 1) * T + first : (2 * t + 1) * T + first + size].reshape(size * 2 * SUB, LANES)
             evens.append(jnp.where(low, v0, pltpu.roll(v1, near, 1)))
             odds.append(jnp.where(low, pltpu.roll(v0, near, 1), v1))
         left = jnp.concatenate([jnp.concatenate(evens, axis=1), jnp.concatenate(odds, axis=1)], axis=0)
@@ -381,22 +414,24 @@
         def times(a, b):
             return jnp.dot(a, b, preferred_element_type=jnp.float32)
 
-        for c in range(C):
-            at_c = slice(c * LANES, (c + 1) * LANES)
-            at_s = slice(length + c * LANES, length + (c + 1) * LANES)
-
-            def product(at):
-                return times(top, ytab[0, :, at]) + (times(rest, ytab[0, :, at]) + times(top, ytab[1, :, at]))
-
-            both = product(at_c).reshape(thick, 2, SUB, LANES), product(at_s).reshape(thick, 2, SUB, LANES)
-            re = both[0][:, 0] + both[1][:, 1]
-            im = both[0][:, 1] - both[1][:, 0]
-            A[p, c * thick : (c + 1) * thick, 0:SUB] = re
-            A[p, c * thick : (c + 1) * thick, SUB : 2 * SUB] = im
-
-    def slab(z):
-        inner = z % thick
-        return z // thick * thick + inner % 2 * (thick // 2) + inner // 2
+        for k in col_order + [0]:
+            c = col ^ k
+            at = pl.ds(pl.multiple_of(c * 2 * LANES, 2 * LANES), 2 * LANES)
+            both = times(top, ytab[0, :, at]) + (times(rest, ytab[0, :, at]) + times(top, ytab[1, :, at]))
+            both = both.reshape(2, size, 2, SUB, 2 * LANES)
+            re = both[:, :, 0, :, :LANES] + both[:, :, 1, :, LANES:]
+            im = both[:, :, 1, :, :LANES] - both[:, :, 0, :, LANES:]
+            for t in range(size):
+                for odd in range(2):
+                    z = c * thick + 2 * (first + t) + odd
+                    if k == 0:
+                        D[p, z, 0:SUB] = re[odd, t]
+                        D[p, z, SUB : 2 * SUB] = im[odd, t]
+                    else:
+                        out[z, 0:SUB] = re[odd, t]
+                        out[z, SUB : 2 * SUB] = im[odd, t]
+            if k != 0:
+                col_part(out, p, k, unit, 2 * first, 2 * size).start()
 
     eight = 8
 
@@ -404,7 +439,7 @@
         for z0 in range(eight):
             items = []
             for z1 in range(eight):
-                at = slab(z1 * eight + z0)
+                at = z1 * eight + z0
                 items.append((D[p, at, 0:SUB], D[p, at, SUB : 2 * SUB]))
             for k0, value in enumerate(fft(items)):
                 angle = 2.0 * math.pi * z0 * k0 / 64
@@ -422,19 +457,13 @@
 
     def finish(p):
         for k in col_order:
-            col_wait(p, k).wait_recv()
+            col_wait(A.at[p], p, k, p).wait_recv()
+        for k in col_order:
+            col_part(A.at[p], p, k, p).wait_send()
         z_step(p)
 
-    def step(p, _):
-        for k in row_order:
-            row_wait(p, k).wait_recv()
-        for k in row_order:
-            row_wait(p, k).wait_send()
-        y_step(p)
-        mine = pl.ds(col * thick, thick)
-        D[p, mine] = A[p, mine]
-        for k in col_order:
-            col_copy(p, k).start()
+    def opening(p, _):
+        y_step(p, A.at[p], p, 0, T)
 
         @pl.when(p >= 1)
         def _():
@@ -442,9 +471,22 @@
 
         return 0
 
+    def step(p, _):
+        for k in row_order:
+            row_wait(p, k, p).wait_recv()
+        for k in row_order:
+            row_wait(p, k, p).wait_send()
+        y_step(p, A.at[p], p, 0, T)
+        finish(p - 1)
+        return 0
+
     def localize():
         for k in row_order:
             row_sum_wait(k).wait_recv()
+        for k in row_order:
+            row_sum(k).wait_send()
+        for k in col_order:
+            col_sum(k).wait_send()
         total = row_parts[0]
         for r in range(1, R):
             total = total + row_parts[r]
@@ -473,19 +515,32 @@
             dist = times(left[i : i + LANES], right)
             localized[i : i + LANES, :] = cov * jnp.exp(-dist / (2.0 * REACH * REACH))
 
-    lax.fori_loop(0, plan.pieces, step, 0)
+    def whole_first(k):
+        return row_copy(
+            A.at[pl.ds(0, H), pl.ds((row ^ k) * T, T)], B.at[pl.ds(0, H), pl.ds((row ^ k) * T, T)], 0, k
+        )
+
+    for k in row_order:
+        whole_first(k).wait_recv()
+    for k in row_order:
+        whole_first(k).wait_send()
+    lax.fori_loop(0, H, opening, 0)
+    lax.fori_loop(H, final, step, 0)
+    for g in range(groups):
+        for k in row_order:
+            row_wait(final, k, final + g, g * ply, ply).wait_recv()
+        y_step(final, last, final + g, g * ply, ply)
+        if g == 0:
+            finish(final - 1)
     localize()
-    finish(plan.pieces - 1)
-    def drain(p, _):
+    for g in range(groups):
+        for k in row_order:
+            row_part(final, k, final + g, g * ply, ply).wait_send()
+    for g in range(groups):
         for k in col_order:
-            col_copy(p, k).wait_send()
-        return 0
-
-    lax.fori_loop(0, plan.pieces, drain, 0)
-    for k in col_order:
-        col_sum(k).wait_send()
-    for k in row_order:
-        row_sum(k).wait_send()
+            col_wait(last, final, k, final + g, g * deep, deep).wait_recv()
+            col_part(last, final, k, final + g, g * deep, deep).wait_send()
+    z_step(final)
 
 
 def exchanged(plan, field, modes, factor):
@@ -499,30 +554,30 @@
             pltpu.VMEM(block, jnp.float32),
             pltpu.VMEM((2 * count, 2 * count), jnp.float32),
         ),
-        in_specs=[
-            pl.BlockSpec(memory_space=pl.ANY),
-            pl.BlockSpec(memory_space=pltpu.VMEM),
-            pl.BlockSpec(memory_space=pltpu.VMEM),
-            pl.BlockSpec(memory_space=pltpu.VMEM),
-        ],
+        in_specs=[pl.BlockSpec(memory_space=pl.ANY)] * 4,
         out_specs=(pl.BlockSpec(memory_space=pltpu.VMEM), pl.BlockSpec(memory_space=pltpu.VMEM)),
         scratch_shapes=[
             pltpu.VMEM(block, jnp.float32),
             pltpu.VMEM(block, jnp.float32),
+            pltpu.VMEM(block[1:], jnp.float32),
             pltpu.VMEM((2, plan.width, plan.width), jnp.bfloat16),
             pltpu.VMEM((2, plan.length, 2 * plan.length), jnp.bfloat16),
             pltpu.VMEM((2, plan.lanes, 2 * count), jnp.bfloat16),
             pltpu.VMEM((2, plan.lanes, plan.width), jnp.float32),
             pltpu.VMEM((plan.depth, 2 * SUB, LANES), jnp.float32),
+            pltpu.VMEM(modes.shape, jnp.int32),
+            pltpu.VMEM(coarse.shape, jnp.float32),
+            pltpu.VMEM(fine.shape, jnp.float32),
             pltpu.VMEM(sums, jnp.float32),
             pltpu.VMEM(sums, jnp.float32),
             pltpu.VMEM((plan.cols,) + sums, jnp.float32),
             pltpu.VMEM((plan.rows,) + sums, jnp.float32),
-            pltpu.SemaphoreType.DMA((plan.pieces,)),
-            pltpu.SemaphoreType.DMA((plan.pieces, plan.rows)),
-            pltpu.SemaphoreType.DMA((plan.pieces,)),
-            pltpu.SemaphoreType.DMA((plan.pieces, plan.cols)),
-            pltpu.SemaphoreType.DMA((2,)),
+            pltpu.SemaphoreType.DMA((plan.pieces + plan.groups,)),
+            pltpu.SemaphoreType.DMA((plan.pieces + plan.groups, plan.rows)),
+            pltpu.SemaphoreType.DMA((plan.pieces + plan.groups,)),
+            pltpu.SemaphoreType.DMA((plan.pieces + plan.groups, plan.cols)),
+            pltpu.SemaphoreType.DMA((plan.groups + 2,)),
+            pltpu.SemaphoreType.DMA((3,)),
             pltpu.SemaphoreType.DMA((2,)),
             pltpu.SemaphoreType.DMA((plan.cols,)),
             pltpu.SemaphoreType.DMA((plan.rows,)),

time: 391 us -> 388 us (level)
  no operation moved by 1% of the time
where the time goes in v3:
time: 388 us
  Pallas kernels  387 us (100%)
    pallas_call x1, Pallas kernels, exchanged(): pl.pallas_call(functools.partial(kernel, plan, factor), out_shape=(pltpu....  381 us

profile of v3, /device:TPU:0, one launch (start us, length us, event | category | flops | bytes accessed | tf_op | source)
XLA Modules:
  0.0 387.8 jit_solution(2844847585690901914)
XLA Ops:
  0.6 380.6 %shard_map.59 = (f32[32,64,16,128]{3,2,1,0:T(8,128)S(1)}, f32[512,512]{1,0:T(8,128)S(1)}) custom-call(f32[64,16,8,512]{3,2,1,0:T(8,128)} %field.1, s32[3,256]{1,0:T(4,128)} %modes_in.1, f32[2,64,512]{2,1,0:T(8,128)} %constant.4.clone.coarse_in, f32[2,8,512]{2,1,0:T(8,128)} %constant.5.clone.fine_in), custom_call_target="tpu_custom_call" | custom-call | tf_op jit(solution)/shard_map/pallas_call | solution.py:551
  381.2 6.4 %shard_map.60 = (f32[64,8,64,128]{3,2,1,0:T(8,128)}, f32[512,512]{1,0:T(8,128)}) custom-call(f32[32,64,16,128]{3,2,1,0:T(8,128)S(1)} %get-tuple-element.6.piled, f32[512,512]{1,0:T(8,128)S(1)} %get-tuple-element.7.square), custom_call_target="tpu_custom_call" | custom-call | tf_op jit(solution)/shard_map/pallas_call | solution.py:602

commit v4 on v3

--- a/solution.py
+++ b/solution.py
@@ -146,6 +146,30 @@
         )
 
 
+EIGHT = 8
+
+
+def z_transform(source, mid, target):
+    for z0 in range(EIGHT):
+        items = []
+        for z1 in range(EIGHT):
+            at = z1 * EIGHT + z0
+            items.append((source[at, 0:SUB], source[at, SUB : 2 * SUB]))
+        for k0, value in enumerate(fft(items)):
+            angle = 2.0 * math.pi * z0 * k0 / 64
+            re, im = value if z0 * k0 == 0 else cmul(value, math.cos(angle), math.sin(angle))
+            mid[k0 * EIGHT + z0, 0:SUB] = re
+            mid[k0 * EIGHT + z0, SUB : 2 * SUB] = im
+    for k0 in range(EIGHT):
+        items = []
+        for z0 in range(EIGHT):
+            at = k0 * EIGHT + z0
+            items.append((mid[at, 0:SUB], mid[at, SUB : 2 * SUB]))
+        for k1, (re, im) in enumerate(fft(items)):
+            target[k0 + EIGHT * k1, pl.ds(0, SUB, stride=2), :] = re
+            target[k0 + EIGHT * k1, pl.ds(1, SUB, stride=2), :] = im
+
+
 def kernel(
     plan, factor, field, modes_in, coarse_in, fine_in, D, localized,
     A, B, last, xtab, ytab, ptab, lines, mid, modes, coarse, fine, part, subtotal, col_parts, row_parts,
@@ -166,6 +190,12 @@
     row_order = list(range(R // 2, R)) + list(range(1, R // 2))
     col_order = list(range(C // 2, C)) + list(range(1, C // 2))
 
+    barrier = pltpu.get_barrier_semaphore()
+    for k in range(1, R):
+        pl.semaphore_signal(barrier, inc=1, device_id=row_peer(k), device_id_type=MESH)
+    for k in range(1, C):
+        pl.semaphore_signal(barrier, inc=1, device_id=col_peer(k), device_id_type=MESH)
+
     def load(m, z, sem):
         at = pl.ds(pl.multiple_of(z * near, near), near)
         return pltpu.make_async_copy(field.at[:, z, m, :], lines.at[m % 2, at, :], in_sem.at[sem])
@@ -180,11 +210,6 @@
     for z in range(thick):
         load(0, z, z // deep).start()
 
-    barrier = pltpu.get_barrier_semaphore()
-    for k in range(1, R):
-        pl.semaphore_signal(barrier, inc=1, device_id=row_peer(k), device_id_type=MESH)
-    for k in range(1, C):
-        pl.semaphore_signal(barrier, inc=1, device_id=col_peer(k), device_id_type=MESH)
     for copy in tables:
         copy.wait()
 
@@ -433,34 +458,12 @@
             if k != 0:
                 col_part(out, p, k, unit, 2 * first, 2 * size).start()
 
-    eight = 8
-
-    def z_step(p):
-        for z0 in range(eight):
-            items = []
-            for z1 in range(eight):
-                at = z1 * eight + z0
-                items.append((D[p, at, 0:SUB], D[p, at, SUB : 2 * SUB]))
-            for k0, value in enumerate(fft(items)):
-                angle = 2.0 * math.pi * z0 * k0 / 64
-                re, im = value if z0 * k0 == 0 else cmul(value, math.cos(angle), math.sin(angle))
-                mid[k0 * eight + z0, 0:SUB] = re
-                mid[k0 * eight + z0, SUB : 2 * SUB] = im
-        for k0 in range(eight):
-            items = []
-            for z0 in range(eight):
-                at = k0 * eight + z0
-                items.append((mid[at, 0:SUB], mid[at, SUB : 2 * SUB]))
-            for k1, (re, im) in enumerate(fft(items)):
-                D[p, k0 + eight * k1, pl.ds(0, SUB, stride=2), :] = re
-                D[p, k0 + eight * k1, pl.ds(1, SUB, stride=2), :] = im
-
     def finish(p):
         for k in col_order:
             col_wait(A.at[p], p, k, p).wait_recv()
         for k in col_order:
             col_part(A.at[p], p, k, p).wait_send()
-        z_step(p)
+        z_transform(D.at[p], mid, D.at[p])
 
     def opening(p, _):
         y_step(p, A.at[p], p, 0, T)
@@ -540,7 +543,6 @@
         for k in col_order:
             col_wait(last, final, k, final + g, g * deep, deep).wait_recv()
             col_part(last, final, k, final + g, g * deep, deep).wait_send()
-    z_step(final)
 
 
 def exchanged(plan, field, modes, factor):
@@ -586,14 +588,21 @@
     )(field, modes, jnp.asarray(coarse), jnp.asarray(fine))
 
 
-def settle(plan, piled, square, whole, localized, sems):
+def settle(plan, piled, square, whole, localized, mid, stage, sems):
     H = plan.parts
-    copies = [pltpu.make_async_copy(square, localized, sems.at[plan.pieces])]
-    for p in range(plan.pieces):
+    final = plan.pieces - 1
+
+    def leave(p, source):
         m, h = p // H, p % H
-        copies.append(pltpu.make_async_copy(piled.at[p], whole.at[:, m, pl.ds(h * 2 * SUB, 2 * SUB), :], sems.at[p]))
+        return pltpu.make_async_copy(source, whole.at[:, m, pl.ds(h * 2 * SUB, 2 * SUB), :], sems.at[p])
+
+    copies = [leave(p, piled.at[p]) for p in range(final)]
+    copies.append(pltpu.make_async_copy(square, localized, sems.at[plan.pieces]))
     for copy in copies:
         copy.start()
+    z_transform(piled.at[final], mid, stage)
+    copies.append(leave(final, stage))
+    copies[-1].start()
     for copy in copies:
         copy.wait()
 
@@ -607,8 +616,12 @@
         ),
         in_specs=[pl.BlockSpec(memory_space=pltpu.VMEM), pl.BlockSpec(memory_space=pltpu.VMEM)],
         out_specs=(pl.BlockSpec(memory_space=pl.ANY), pl.BlockSpec(memory_space=pl.ANY)),
-        scratch_shapes=[pltpu.SemaphoreType.DMA((plan.pieces + 1,))],
-        compiler_params=pltpu.CompilerParams(vmem_limit_bytes=1 << 20),
+        scratch_shapes=[
+            pltpu.VMEM((plan.depth, 2 * SUB, LANES), jnp.float32),
+            pltpu.VMEM((plan.depth, 2 * SUB, LANES), jnp.float32),
+            pltpu.SemaphoreType.DMA((plan.pieces + 1,)),
+        ],
+        compiler_params=pltpu.CompilerParams(vmem_limit_bytes=1 << 22),
     )(pltpu.with_memory_space_constraint(piled, pltpu.VMEM), pltpu.with_memory_space_constraint(square, pltpu.VMEM))
 
 

time: 388 us -> 388 us (level)
  no operation moved by 1% of the time
where the time goes in v4:
time: 388 us; the launch traced here: 387 us
  Pallas kernels  387 us (100%)
    pallas_call x1, Pallas kernels, exchanged(): pl.pallas_call(functools.partial(kernel, plan, factor), out_shape=(pltpu....  380 us

profile of v4, /device:TPU:0, one launch (start us, length us, event | category | flops | bytes accessed | tf_op | source)
XLA Modules:
  0.0 387.5 jit_solution(6149344676226843345)
XLA Ops:
  0.6 380.3 %shard_map.59 = (f32[32,64,16,128]{3,2,1,0:T(8,128)S(1)}, f32[512,512]{1,0:T(8,128)S(1)}) custom-call(f32[64,16,8,512]{3,2,1,0:T(8,128)} %field.1, s32[3,256]{1,0:T(4,128)} %modes_in.1, f32[2,64,512]{2,1,0:T(8,128)} %constant.4.clone.coarse_in, f32[2,8,512]{2,1,0:T(8,128)} %constant.5.clone.fine_in), custom_call_target="tpu_custom_call" | custom-call | tf_op jit(solution)/shard_map/pallas_call | solution.py:553
  380.9 6.4 %shard_map.60 = (f32[64,8,64,128]{3,2,1,0:T(8,128)}, f32[512,512]{1,0:T(8,128)}) custom-call(f32[32,64,16,128]{3,2,1,0:T(8,128)S(1)} %get-tuple-element.6.piled, f32[512,512]{1,0:T(8,128)S(1)} %get-tuple-element.7.square), custom_call_target="tpu_custom_call" | custom-call | tf_op jit(solution)/shard_map/pallas_call | solution.py:611
